TPU v7x, 32 devices: a whole 2x2x4 slice. The times are simulated.
32 devices in a mesh: lat: 4 (over y, x), lon: 8 (over z, core).
Axes of the slice: x: 2, y: 2, z: 4, core: 2. Of those that a mesh axis runs over, the one named last changes fastest.
Arguments:
- transport: bfloat16 [48, 512, 3072], P(None, 'lat', 'lon'), may hold values from -0.0625 to 0.0625
- sigma_class: int32 [48, 512, 3072], P(None, 'lat', 'lon'), may hold values from 0 to 199
- basin_id: int32 [512, 3072], P('lat', 'lon'), may hold values from 0 to 3
- depth_levels: int32 [512, 3072], P('lat', 'lon'), may hold values from 0 to 48
Outputs:
- overturning: bfloat16 [4, 200, 512], replicated
Inputs may be any that keep to these rules, and one draw needn't show every extreme that they name: `depth_levels`: 0 marks a land column.
All inputs are finite; a program needn't handle non-finite values.
Results may differ from a plain program's by a relative error of at most 0.001.
Values may be sent and summed in bfloat16 or wider, within the bound.
A program may use at most 64 MiB of HBM per device.

v0:
```python
import jax
import jax.numpy as jnp
from jax import lax
from jax.sharding import PartitionSpec as P

CLASSES = 200
BASINS = 4


def bin_rows(transport, sigma_class, basin_id, depth_levels):
    depth_count, row_count, col_count = sigma_class.shape
    block_rows = 8
    block_count = row_count // block_rows
    cell_count = depth_count * col_count
    level_index = lax.broadcasted_iota(jnp.int32, (block_rows, depth_count, col_count), 1)
    class_iota = lax.broadcasted_iota(jnp.int32, (1, CLASSES, 1), 1)
    basin_iota = lax.broadcasted_iota(jnp.int32, (1, BASINS, 1), 1)

    def one_block(start):
        flow = jnp.transpose(lax.dynamic_slice_in_dim(transport, start, block_rows, 1), (1, 0, 2))
        klass = jnp.transpose(
            lax.dynamic_slice_in_dim(sigma_class, start, block_rows, 1), (1, 0, 2)
        )
        basin = lax.dynamic_slice_in_dim(basin_id, start, block_rows, 0)
        depth = lax.dynamic_slice_in_dim(depth_levels, start, block_rows, 0)
        wet_cells = level_index < depth[:, None, :]
        masked = jnp.where(wet_cells, flow, jnp.zeros_like(flow)).reshape(block_rows, 1, cell_count)
        basin_cells = jnp.broadcast_to(
            basin[:, None, :], (block_rows, depth_count, col_count)
        ).reshape(block_rows, 1, cell_count)
        basin_flow = jnp.where(basin_cells == basin_iota, masked, jnp.zeros_like(masked))
        class_hot = (klass.reshape(block_rows, 1, cell_count) == class_iota).astype(jnp.bfloat16)
        return jnp.einsum("rcn,rbn->rbc", class_hot, basin_flow, preferred_element_type=jnp.float32)

    starts = jnp.arange(block_count) * block_rows
    tables = lax.map(one_block, starts)
    return jnp.transpose(tables.reshape(row_count, BASINS, CLASSES), (1, 2, 0))


def body(transport, sigma_class, basin_id, depth_levels):
    table = bin_rows(transport, sigma_class, basin_id, depth_levels)
    shares = lax.psum_scatter(table, "lon", scatter_dimension=2, tiled=True)
    overturn = jnp.cumsum(shares, axis=1).astype(jnp.bfloat16)
    return lax.all_gather(overturn, ("lat", "lon"), axis=2, tiled=True)


def solution(mesh):
    placed = (P(None, "lat", "lon"), P(None, "lat", "lon"), P("lat", "lon"), P("lat", "lon"))
    return jax.shard_map(body, mesh=mesh, in_specs=placed, out_specs=P(), check_vma=False)
```

profile of v0, /device:TPU:0, one launch (start us, length us, event | category | flops | bytes accessed | tf_op | source)
XLA Modules:
  0.0 477.0 jit_solution(9716318747459529076)
XLA Ops:
  6.5 380.7 %while.11 = (s32[]{:T(128)}, f32[16,8,4,200]{3,2,1,0:T(4,128)S(1)}, s32[16]{0:T(128)S(1)}, s32[128,384]{1,0:T(8,128)}, s32[128,384]{1,0:T(8,128)}, /*index=5*/bf...) while((s32[]{:T(128)}, f32[16,8,4,200]{3,2,1,0:T(4,128)S(1)}, ...), condition=%wide.region_1.2_spmd.clone, body=%wide.region_0.1_spmd.clone.sunk | while | flops 266895360 | bytes 3940515 | solution.py:36
  9.3 0.8 constant_dynamic-slice_fusion.6
  10.1 1.2 fusion.29
  11.3 1.4 constant_dynamic-slice_fusion.5
  12.7 17.7 %fusion.30 = f32[16,8,4,200]{3,2,1,0:T(4,128)S(1)} fusion(f32[16,8,4,200]{3,2,1,0:T(4,128)S(1)} %get-tuple-element.150, s32[]{:T(128)} %get-tuple-element.149, s32[8,18432]{1,0:T(8,128)S(1)} %bitcast.46, s32[8,18432]{1,0:T(8,128)S(1)} %bitcast.45, bf16[8,18432]{1,0:T(8,128)(2,1)S(1)} %bitcast.47), kind=kOutput, calls=%fused_computation.10.clone.1 | convolution fusion | flops 266600448 | bytes 1507332 | tf_op jit(solution)/shard_map/while/body/eval_jaxpr/rcn,rbn->rbc/dot_general | solution.py:33
  33.1 0.8 constant_dynamic-slice_fusion.6
  33.9 1.2 fusion.29
  35.1 1.4 constant_dynamic-slice_fusion.5
  36.5 17.7 %fusion.30 = f32[16,8,4,200]{3,2,1,0:T(4,128)S(1)} fusion(f32[16,8,4,200]{3,2,1,0:T(4,128)S(1)} %get-tuple-element.150, s32[]{:T(128)} %get-tuple-element.149, s32[8,18432]{1,0:T(8,128)S(1)} %bitcast.46, s32[8,18432]{1,0:T(8,128)S(1)} %bitcast.45, bf16[8,18432]{1,0:T(8,128)(2,1)S(1)} %bitcast.47), kind=kOutput, calls=%fused_computation.10.clone.1 | convolution fusion | flops 266600448 | bytes 1507332 | tf_op jit(solution)/shard_map/while/body/eval_jaxpr/rcn,rbn->rbc/dot_general | solution.py:33
  56.9 0.8 constant_dynamic-slice_fusion.6
  57.7 1.2 fusion.29
  58.9 1.4 constant_dynamic-slice_fusion.5
  60.3 17.7 %fusion.30 = f32[16,8,4,200]{3,2,1,0:T(4,128)S(1)} fusion(f32[16,8,4,200]{3,2,1,0:T(4,128)S(1)} %get-tuple-element.150, s32[]{:T(128)} %get-tuple-element.149, s32[8,18432]{1,0:T(8,128)S(1)} %bitcast.46, s32[8,18432]{1,0:T(8,128)S(1)} %bitcast.45, bf16[8,18432]{1,0:T(8,128)(2,1)S(1)} %bitcast.47), kind=kOutput, calls=%fused_computation.10.clone.1 | convolution fusion | flops 266600448 | bytes 1507332 | tf_op jit(solution)/shard_map/while/body/eval_jaxpr/rcn,rbn->rbc/dot_general | solution.py:33
  80.7 0.8 constant_dynamic-slice_fusion.6
  81.5 1.2 fusion.29
  82.7 1.4 constant_dynamic-slice_fusion.5
  84.1 17.7 %fusion.30 = f32[16,8,4,200]{3,2,1,0:T(4,128)S(1)} fusion(f32[16,8,4,200]{3,2,1,0:T(4,128)S(1)} %get-tuple-element.150, s32[]{:T(128)} %get-tuple-element.149, s32[8,18432]{1,0:T(8,128)S(1)} %bitcast.46, s32[8,18432]{1,0:T(8,128)S(1)} %bitcast.45, bf16[8,18432]{1,0:T(8,128)(2,1)S(1)} %bitcast.47), kind=kOutput, calls=%fused_computation.10.clone.1 | convolution fusion | flops 266600448 | bytes 1507332 | tf_op jit(solution)/shard_map/while/body/eval_jaxpr/rcn,rbn->rbc/dot_general | solution.py:33
  104.5 0.8 constant_dynamic-slice_fusion.6
  105.3 1.2 fusion.29
  106.6 1.4 constant_dynamic-slice_fusion.5
  107.9 17.7 %fusion.30 = f32[16,8,4,200]{3,2,1,0:T(4,128)S(1)} fusion(f32[16,8,4,200]{3,2,1,0:T(4,128)S(1)} %get-tuple-element.150, s32[]{:T(128)} %get-tuple-element.149, s32[8,18432]{1,0:T(8,128)S(1)} %bitcast.46, s32[8,18432]{1,0:T(8,128)S(1)} %bitcast.45, bf16[8,18432]{1,0:T(8,128)(2,1)S(1)} %bitcast.47), kind=kOutput, calls=%fused_computation.10.clone.1 | convolution fusion | flops 266600448 | bytes 1507332 | tf_op jit(solution)/shard_map/while/body/eval_jaxpr/rcn,rbn->rbc/dot_general | solution.py:33
  128.4 0.8 constant_dynamic-slice_fusion.6
  129.1 1.2 fusion.29
  130.4 1.4 constant_dynamic-slice_fusion.5
  131.7 17.7 %fusion.30 = f32[16,8,4,200]{3,2,1,0:T(4,128)S(1)} fusion(f32[16,8,4,200]{3,2,1,0:T(4,128)S(1)} %get-tuple-element.150, s32[]{:T(128)} %get-tuple-element.149, s32[8,18432]{1,0:T(8,128)S(1)} %bitcast.46, s32[8,18432]{1,0:T(8,128)S(1)} %bitcast.45, bf16[8,18432]{1,0:T(8,128)(2,1)S(1)} %bitcast.47), kind=kOutput, calls=%fused_computation.10.clone.1 | convolution fusion | flops 266600448 | bytes 1507332 | tf_op jit(solution)/shard_map/while/body/eval_jaxpr/rcn,rbn->rbc/dot_general | solution.py:33
  152.2 0.8 constant_dynamic-slice_fusion.6
  152.9 1.2 fusion.29
  154.2 1.4 constant_dynamic-slice_fusion.5
  155.5 17.7 %fusion.30 = f32[16,8,4,200]{3,2,1,0:T(4,128)S(1)} fusion(f32[16,8,4,200]{3,2,1,0:T(4,128)S(1)} %get-tuple-element.150, s32[]{:T(128)} %get-tuple-element.149, s32[8,18432]{1,0:T(8,128)S(1)} %bitcast.46, s32[8,18432]{1,0:T(8,128)S(1)} %bitcast.45, bf16[8,18432]{1,0:T(8,128)(2,1)S(1)} %bitcast.47), kind=kOutput, calls=%fused_computation.10.clone.1 | convolution fusion | flops 266600448 | bytes 1507332 | tf_op jit(solution)/shard_map/while/body/eval_jaxpr/rcn,rbn->rbc/dot_general | solution.py:33
  176.0 0.8 constant_dynamic-slice_fusion.6
  176.8 1.2 fusion.29
  178.0 1.4 constant_dynamic-slice_fusion.5
  179.4 17.7 %fusion.30 = f32[16,8,4,200]{3,2,1,0:T(4,128)S(1)} fusion(f32[16,8,4,200]{3,2,1,0:T(4,128)S(1)} %get-tuple-element.150, s32[]{:T(128)} %get-tuple-element.149, s32[8,18432]{1,0:T(8,128)S(1)} %bitcast.46, s32[8,18432]{1,0:T(8,128)S(1)} %bitcast.45, bf16[8,18432]{1,0:T(8,128)(2,1)S(1)} %bitcast.47), kind=kOutput, calls=%fused_computation.10.clone.1 | convolution fusion | flops 266600448 | bytes 1507332 | tf_op jit(solution)/shard_map/while/body/eval_jaxpr/rcn,rbn->rbc/dot_general | solution.py:33
  199.8 0.8 constant_dynamic-slice_fusion.6
  200.6 1.2 fusion.29
  201.8 1.4 constant_dynamic-slice_fusion.5
  203.2 17.7 %fusion.30 = f32[16,8,4,200]{3,2,1,0:T(4,128)S(1)} fusion(f32[16,8,4,200]{3,2,1,0:T(4,128)S(1)} %get-tuple-element.150, s32[]{:T(128)} %get-tuple-element.149, s32[8,18432]{1,0:T(8,128)S(1)} %bitcast.46, s32[8,18432]{1,0:T(8,128)S(1)} %bitcast.45, bf16[8,18432]{1,0:T(8,128)(2,1)S(1)} %bitcast.47), kind=kOutput, calls=%fused_computation.10.clone.1 | convolution fusion | flops 266600448 | bytes 1507332 | tf_op jit(solution)/shard_map/while/body/eval_jaxpr/rcn,rbn->rbc/dot_general | solution.py:33
  224.4 1.2 fusion.29
  225.6 1.4 constant_dynamic-slice_fusion.5
  227.0 17.7 %fusion.30 = f32[16,8,4,200]{3,2,1,0:T(4,128)S(1)} fusion(f32[16,8,4,200]{3,2,1,0:T(4,128)S(1)} %get-tuple-element.150, s32[]{:T(128)} %get-tuple-element.149, s32[8,18432]{1,0:T(8,128)S(1)} %bitcast.46, s32[8,18432]{1,0:T(8,128)S(1)} %bitcast.45, bf16[8,18432]{1,0:T(8,128)(2,1)S(1)} %bitcast.47), kind=kOutput, calls=%fused_computation.10.clone.1 | convolution fusion | flops 266600448 | bytes 1507332 | tf_op jit(solution)/shard_map/while/body/eval_jaxpr/rcn,rbn->rbc/dot_general | solution.py:33
  248.2 1.2 fusion.29
  249.4 1.4 constant_dynamic-slice_fusion.5
  250.8 17.7 %fusion.30 = f32[16,8,4,200]{3,2,1,0:T(4,128)S(1)} fusion(f32[16,8,4,200]{3,2,1,0:T(4,128)S(1)} %get-tuple-element.150, s32[]{:T(128)} %get-tuple-element.149, s32[8,18432]{1,0:T(8,128)S(1)} %bitcast.46, s32[8,18432]{1,0:T(8,128)S(1)} %bitcast.45, bf16[8,18432]{1,0:T(8,128)(2,1)S(1)} %bitcast.47), kind=kOutput, calls=%fused_computation.10.clone.1 | convolution fusion | flops 266600448 | bytes 1507332 | tf_op jit(solution)/shard_map/while/body/eval_jaxpr/rcn,rbn->rbc/dot_general | solution.py:33
  272.0 1.2 fusion.29
  273.3 1.4 constant_dynamic-slice_fusion.5
  274.6 17.7 %fusion.30 = f32[16,8,4,200]{3,2,1,0:T(4,128)S(1)} fusion(f32[16,8,4,200]{3,2,1,0:T(4,128)S(1)} %get-tuple-element.150, s32[]{:T(128)} %get-tuple-element.149, s32[8,18432]{1,0:T(8,128)S(1)} %bitcast.46, s32[8,18432]{1,0:T(8,128)S(1)} %bitcast.45, bf16[8,18432]{1,0:T(8,128)(2,1)S(1)} %bitcast.47), kind=kOutput, calls=%fused_computation.10.clone.1 | convolution fusion | flops 266600448 | bytes 1507332 | tf_op jit(solution)/shard_map/while/body/eval_jaxpr/rcn,rbn->rbc/dot_general | solution.py:33
  295.8 1.2 fusion.29
  297.1 1.4 constant_dynamic-slice_fusion.5
  298.4 17.7 %fusion.30 = f32[16,8,4,200]{3,2,1,0:T(4,128)S(1)} fusion(f32[16,8,4,200]{3,2,1,0:T(4,128)S(1)} %get-tuple-element.150, s32[]{:T(128)} %get-tuple-element.149, s32[8,18432]{1,0:T(8,128)S(1)} %bitcast.46, s32[8,18432]{1,0:T(8,128)S(1)} %bitcast.45, bf16[8,18432]{1,0:T(8,128)(2,1)S(1)} %bitcast.47), kind=kOutput, calls=%fused_computation.10.clone.1 | convolution fusion | flops 266600448 | bytes 1507332 | tf_op jit(solution)/shard_map/while/body/eval_jaxpr/rcn,rbn->rbc/dot_general | solution.py:33
  319.6 1.2 fusion.29
  320.9 1.4 constant_dynamic-slice_fusion.5
  322.2 17.7 %fusion.30 = f32[16,8,4,200]{3,2,1,0:T(4,128)S(1)} fusion(f32[16,8,4,200]{3,2,1,0:T(4,128)S(1)} %get-tuple-element.150, s32[]{:T(128)} %get-tuple-element.149, s32[8,18432]{1,0:T(8,128)S(1)} %bitcast.46, s32[8,18432]{1,0:T(8,128)S(1)} %bitcast.45, bf16[8,18432]{1,0:T(8,128)(2,1)S(1)} %bitcast.47), kind=kOutput, calls=%fused_computation.10.clone.1 | convolution fusion | flops 266600448 | bytes 1507332 | tf_op jit(solution)/shard_map/while/body/eval_jaxpr/rcn,rbn->rbc/dot_general | solution.py:33
  343.5 1.2 fusion.29
  344.7 1.4 constant_dynamic-slice_fusion.5
  346.1 17.7 %fusion.30 = f32[16,8,4,200]{3,2,1,0:T(4,128)S(1)} fusion(f32[16,8,4,200]{3,2,1,0:T(4,128)S(1)} %get-tuple-element.150, s32[]{:T(128)} %get-tuple-element.149, s32[8,18432]{1,0:T(8,128)S(1)} %bitcast.46, s32[8,18432]{1,0:T(8,128)S(1)} %bitcast.45, bf16[8,18432]{1,0:T(8,128)(2,1)S(1)} %bitcast.47), kind=kOutput, calls=%fused_computation.10.clone.1 | convolution fusion | flops 266600448 | bytes 1507332 | tf_op jit(solution)/shard_map/while/body/eval_jaxpr/rcn,rbn->rbc/dot_general | solution.py:33
  367.2 1.1 fusion.29
  368.4 1.1 constant_dynamic-slice_fusion.5
  369.5 17.7 %fusion.30 = f32[16,8,4,200]{3,2,1,0:T(4,128)S(1)} fusion(f32[16,8,4,200]{3,2,1,0:T(4,128)S(1)} %get-tuple-element.150, s32[]{:T(128)} %get-tuple-element.149, s32[8,18432]{1,0:T(8,128)S(1)} %bitcast.46, s32[8,18432]{1,0:T(8,128)S(1)} %bitcast.45, bf16[8,18432]{1,0:T(8,128)(2,1)S(1)} %bitcast.47), kind=kOutput, calls=%fused_computation.10.clone.1 | convolution fusion | flops 266600448 | bytes 1507332 | tf_op jit(solution)/shard_map/while/body/eval_jaxpr/rcn,rbn->rbc/dot_general | solution.py:33
  387.2 0.9 copy.18
  388.1 34.0 %reduce-scatter.2.cloned.1.call-done = f32[4,200,16]{1,2,0:T(8,128)} async-done(((f32[4,200,128]{1,2,0:T(8,128)}), f32[4,200,16]{1,2,0:T(8,128)}) %reduce-scatter.2.cloned.1.call-update) | async-done | bytes 51216 | tf_op jit(solution)/shard_map/reduce_scatter | solution.py:42
  422.2 0.8 copy_bitcast_fusion.1
  423.0 2.3 reduce-window.6
  425.6 43.3 %all_gather.3 = bf16[4,200,512]{1,2,0:T(8,128)(2,1)S(1)} all-gather(bf16[4,200,16]{1,2,0:T(8,128)(2,1)S(1)} %bitcast.50), channel_id=1, replica_groups=mesh['lat'=4,'lon'=8] {'lat','lon'}, dimensions={2}, use_global_device_ids=true | all-gather | bytes 844800 | tf_op jit(solution)/shard_map/all_gather | solution.py:44
  468.9 1.2 copy.12
  (49 shorter events, 17.0 us)
Async XLA Ops:
  6.5 415.6 %reduce-scatter.2.cloned.1.call-start = ((), (), s32[]{:S(2)}) async-start(), calls=%async_computation.1 | async-start | bytes 589824 | tf_op jit(solution)/shard_map/reduce_scatter | solution.py:42
Sparse Core Ops, SparseCore 0:
  388.3 33.8 reduce-scatter.1
where the time goes:
time: 480 us; the launch traced here: 477 us
  matrix products  283 us (59%)
  local copies, waits for them, and re-layouts  48.3 us (10%)
  blocking collectives  43.3 us (9%)
  waiting for transfers between devices  34 us (7%)
  loops' own time  33.4 us (7%)
  other arithmetic  21.5 us (4%)
  between operations  13.4 us (3%)
    dot_general x16, matrix products, one_block(): jnp.einsum('rcn,rbn->rbc', class_hot, basin_flow, preferred_element_type=...  283 us
    all_gather x1, blocking collectives, body(): return lax.all_gather(overturn, ('lat', 'lon'), axis=2, tiled=True)  43.3 us
    reduce_scatter x1, waiting for transfers between devices, body(): shares = lax.psum_scatter(table, 'lon', scatter_dimension=2, tiled=True)  34 us
    another operation x1, loops' own time, bin_rows(): tables = lax.map(one_block, starts)  33.4 us
    dynamic_slice x16, local copies, waits for them, and re-layouts, one_block(): lax.dynamic_slice_in_dim(sigma_class, start, block_rows, 1)  21.4 us
    select_n x16, other arithmetic, one_block(): jnp.where(wet_cells, flow, jnp.zeros_like(flow))  19.1 us
    dynamic_slice x16, local copies, waits for them, and re-layouts, one_block(): depth = lax.dynamic_slice_in_dim(depth_levels, start, block_rows, 0)  12.3 us
    dynamic_slice x16, local copies, waits for them, and re-layouts, bin_rows(): tables = lax.map(one_block, starts)  10.7 us
  transfers between devices with their start and end apart: 1, of which 1 were waited for; matrix products, arithmetic and copies ran while one was open for 0% of the time, Pallas kernels for 0%

commit v1 on v0

--- a/solution.py
+++ b/solution.py
@@ -41,7 +41,7 @@
     table = bin_rows(transport, sigma_class, basin_id, depth_levels)
     shares = lax.psum_scatter(table, "lon", scatter_dimension=2, tiled=True)
     overturn = jnp.cumsum(shares, axis=1).astype(jnp.bfloat16)
-    return lax.all_gather(overturn, ("lat", "lon"), axis=2, tiled=True)
+    return jnp.concatenate(lax.all_gather(overturn, ("lat", "lon")), axis=2)
 
 
 def solution(mesh):

time: 480 us -> 480 us (level)
  no operation moved by 1% of the time
where the time goes in v1:
time: 480 us; the launch traced here: 477 us
  matrix products  283 us (59%)
  local copies, waits for them, and re-layouts  48.3 us (10%)
  blocking collectives  43.3 us (9%)
  waiting for transfers between devices  34 us (7%)
  loops' own time  33.4 us (7%)
  other arithmetic  21.5 us (4%)
  between operations  13.4 us (3%)
    dot_general x16, matrix products, one_block(): jnp.einsum('rcn,rbn->rbc', class_hot, basin_flow, preferred_element_type=...  283 us
    all_gather x1, blocking collectives, body(): return jnp.concatenate(lax.all_gather(overturn, ('lat', 'lon')), axis=2)  43.3 us
    reduce_scatter x1, waiting for transfers between devices, body(): shares = lax.psum_scatter(table, 'lon', scatter_dimension=2, tiled=True)  34 us
    another operation x1, loops' own time, bin_rows(): tables = lax.map(one_block, starts)  33.4 us
    dynamic_slice x16, local copies, waits for them, and re-layouts, one_block(): lax.dynamic_slice_in_dim(sigma_class, start, block_rows, 1)  21.4 us
    select_n x16, other arithmetic, one_block(): jnp.where(wet_cells, flow, jnp.zeros_like(flow))  19.1 us
    dynamic_slice x16, local copies, waits for them, and re-layouts, one_block(): depth = lax.dynamic_slice_in_dim(depth_levels, start, block_rows, 0)  12.3 us
    dynamic_slice x16, local copies, waits for them, and re-layouts, bin_rows(): tables = lax.map(one_block, starts)  10.7 us
  transfers between devices with their start and end apart: 1, of which 1 were waited for; matrix products, arithmetic and copies ran while one was open for 0% of the time, Pallas kernels for 0%

profile of v1, /device:TPU:0, one launch (start us, length us, event | category | flops | bytes accessed | tf_op | source)
XLA Modules:
  0.0 477.1 jit_solution(13743657388425474255)
XLA Ops:
  6.5 380.7 %while.11 = (s32[]{:T(128)}, f32[16,8,4,200]{3,2,1,0:T(4,128)S(1)}, s32[16]{0:T(128)S(1)}, s32[128,384]{1,0:T(8,128)}, s32[128,384]{1,0:T(8,128)}, /*index=5*/bf...) while((s32[]{:T(128)}, f32[16,8,4,200]{3,2,1,0:T(4,128)S(1)}, ...), condition=%wide.region_1.2_spmd.clone, body=%wide.region_0.1_spmd.clone.sunk | while | flops 266895360 | bytes 3940515 | solution.py:36
  9.3 0.8 constant_dynamic-slice_fusion.6
  10.1 1.2 fusion.29
  11.3 1.4 constant_dynamic-slice_fusion.5
  12.7 17.7 %fusion.30 = f32[16,8,4,200]{3,2,1,0:T(4,128)S(1)} fusion(f32[16,8,4,200]{3,2,1,0:T(4,128)S(1)} %get-tuple-element.150, s32[]{:T(128)} %get-tuple-element.149, s32[8,18432]{1,0:T(8,128)S(1)} %bitcast.50, s32[8,18432]{1,0:T(8,128)S(1)} %bitcast.49, bf16[8,18432]{1,0:T(8,128)(2,1)S(1)} %bitcast.51), kind=kOutput, calls=%fused_computation.10.clone.1 | convolution fusion | flops 266600448 | bytes 1507332 | tf_op jit(solution)/shard_map/while/body/eval_jaxpr/rcn,rbn->rbc/dot_general | solution.py:33
  33.1 0.8 constant_dynamic-slice_fusion.6
  33.9 1.2 fusion.29
  35.1 1.4 constant_dynamic-slice_fusion.5
  36.5 17.7 %fusion.30 = f32[16,8,4,200]{3,2,1,0:T(4,128)S(1)} fusion(f32[16,8,4,200]{3,2,1,0:T(4,128)S(1)} %get-tuple-element.150, s32[]{:T(128)} %get-tuple-element.149, s32[8,18432]{1,0:T(8,128)S(1)} %bitcast.50, s32[8,18432]{1,0:T(8,128)S(1)} %bitcast.49, bf16[8,18432]{1,0:T(8,128)(2,1)S(1)} %bitcast.51), kind=kOutput, calls=%fused_computation.10.clone.1 | convolution fusion | flops 266600448 | bytes 1507332 | tf_op jit(solution)/shard_map/while/body/eval_jaxpr/rcn,rbn->rbc/dot_general | solution.py:33
  56.9 0.8 constant_dynamic-slice_fusion.6
  57.7 1.2 fusion.29
  58.9 1.4 constant_dynamic-slice_fusion.5
  60.3 17.7 %fusion.30 = f32[16,8,4,200]{3,2,1,0:T(4,128)S(1)} fusion(f32[16,8,4,200]{3,2,1,0:T(4,128)S(1)} %get-tuple-element.150, s32[]{:T(128)} %get-tuple-element.149, s32[8,18432]{1,0:T(8,128)S(1)} %bitcast.50, s32[8,18432]{1,0:T(8,128)S(1)} %bitcast.49, bf16[8,18432]{1,0:T(8,128)(2,1)S(1)} %bitcast.51), kind=kOutput, calls=%fused_computation.10.clone.1 | convolution fusion | flops 266600448 | bytes 1507332 | tf_op jit(solution)/shard_map/while/body/eval_jaxpr/rcn,rbn->rbc/dot_general | solution.py:33
  80.7 0.8 constant_dynamic-slice_fusion.6
  81.5 1.2 fusion.29
  82.7 1.4 constant_dynamic-slice_fusion.5
  84.1 17.7 %fusion.30 = f32[16,8,4,200]{3,2,1,0:T(4,128)S(1)} fusion(f32[16,8,4,200]{3,2,1,0:T(4,128)S(1)} %get-tuple-element.150, s32[]{:T(128)} %get-tuple-element.149, s32[8,18432]{1,0:T(8,128)S(1)} %bitcast.50, s32[8,18432]{1,0:T(8,128)S(1)} %bitcast.49, bf16[8,18432]{1,0:T(8,128)(2,1)S(1)} %bitcast.51), kind=kOutput, calls=%fused_computation.10.clone.1 | convolution fusion | flops 266600448 | bytes 1507332 | tf_op jit(solution)/shard_map/while/body/eval_jaxpr/rcn,rbn->rbc/dot_general | solution.py:33
  104.5 0.8 constant_dynamic-slice_fusion.6
  105.3 1.2 fusion.29
  106.6 1.4 constant_dynamic-slice_fusion.5
  107.9 17.7 %fusion.30 = f32[16,8,4,200]{3,2,1,0:T(4,128)S(1)} fusion(f32[16,8,4,200]{3,2,1,0:T(4,128)S(1)} %get-tuple-element.150, s32[]{:T(128)} %get-tuple-element.149, s32[8,18432]{1,0:T(8,128)S(1)} %bitcast.50, s32[8,18432]{1,0:T(8,128)S(1)} %bitcast.49, bf16[8,18432]{1,0:T(8,128)(2,1)S(1)} %bitcast.51), kind=kOutput, calls=%fused_computation.10.clone.1 | convolution fusion | flops 266600448 | bytes 1507332 | tf_op jit(solution)/shard_map/while/body/eval_jaxpr/rcn,rbn->rbc/dot_general | solution.py:33
  128.4 0.8 constant_dynamic-slice_fusion.6
  129.1 1.2 fusion.29
  130.4 1.4 constant_dynamic-slice_fusion.5
  131.7 17.7 %fusion.30 = f32[16,8,4,200]{3,2,1,0:T(4,128)S(1)} fusion(f32[16,8,4,200]{3,2,1,0:T(4,128)S(1)} %get-tuple-element.150, s32[]{:T(128)} %get-tuple-element.149, s32[8,18432]{1,0:T(8,128)S(1)} %bitcast.50, s32[8,18432]{1,0:T(8,128)S(1)} %bitcast.49, bf16[8,18432]{1,0:T(8,128)(2,1)S(1)} %bitcast.51), kind=kOutput, calls=%fused_computation.10.clone.1 | convolution fusion | flops 266600448 | bytes 1507332 | tf_op jit(solution)/shard_map/while/body/eval_jaxpr/rcn,rbn->rbc/dot_general | solution.py:33
  152.2 0.8 constant_dynamic-slice_fusion.6
  152.9 1.2 fusion.29
  154.2 1.4 constant_dynamic-slice_fusion.5
  155.5 17.7 %fusion.30 = f32[16,8,4,200]{3,2,1,0:T(4,128)S(1)} fusion(f32[16,8,4,200]{3,2,1,0:T(4,128)S(1)} %get-tuple-element.150, s32[]{:T(128)} %get-tuple-element.149, s32[8,18432]{1,0:T(8,128)S(1)} %bitcast.50, s32[8,18432]{1,0:T(8,128)S(1)} %bitcast.49, bf16[8,18432]{1,0:T(8,128)(2,1)S(1)} %bitcast.51), kind=kOutput, calls=%fused_computation.10.clone.1 | convolution fusion | flops 266600448 | bytes 1507332 | tf_op jit(solution)/shard_map/while/body/eval_jaxpr/rcn,rbn->rbc/dot_general | solution.py:33
  176.0 0.8 constant_dynamic-slice_fusion.6
  176.8 1.2 fusion.29
  178.0 1.4 constant_dynamic-slice_fusion.5
  179.4 17.7 %fusion.30 = f32[16,8,4,200]{3,2,1,0:T(4,128)S(1)} fusion(f32[16,8,4,200]{3,2,1,0:T(4,128)S(1)} %get-tuple-element.150, s32[]{:T(128)} %get-tuple-element.149, s32[8,18432]{1,0:T(8,128)S(1)} %bitcast.50, s32[8,18432]{1,0:T(8,128)S(1)} %bitcast.49, bf16[8,18432]{1,0:T(8,128)(2,1)S(1)} %bitcast.51), kind=kOutput, calls=%fused_computation.10.clone.1 | convolution fusion | flops 266600448 | bytes 1507332 | tf_op jit(solution)/shard_map/while/body/eval_jaxpr/rcn,rbn->rbc/dot_general | solution.py:33
  199.8 0.8 constant_dynamic-slice_fusion.6
  200.6 1.2 fusion.29
  201.8 1.4 constant_dynamic-slice_fusion.5
  203.2 17.7 %fusion.30 = f32[16,8,4,200]{3,2,1,0:T(4,128)S(1)} fusion(f32[16,8,4,200]{3,2,1,0:T(4,128)S(1)} %get-tuple-element.150, s32[]{:T(128)} %get-tuple-element.149, s32[8,18432]{1,0:T(8,128)S(1)} %bitcast.50, s32[8,18432]{1,0:T(8,128)S(1)} %bitcast.49, bf16[8,18432]{1,0:T(8,128)(2,1)S(1)} %bitcast.51), kind=kOutput, calls=%fused_computation.10.clone.1 | convolution fusion | flops 266600448 | bytes 1507332 | tf_op jit(solution)/shard_map/while/body/eval_jaxpr/rcn,rbn->rbc/dot_general | solution.py:33
  224.4 1.2 fusion.29
  225.6 1.4 constant_dynamic-slice_fusion.5
  227.0 17.7 %fusion.30 = f32[16,8,4,200]{3,2,1,0:T(4,128)S(1)} fusion(f32[16,8,4,200]{3,2,1,0:T(4,128)S(1)} %get-tuple-element.150, s32[]{:T(128)} %get-tuple-element.149, s32[8,18432]{1,0:T(8,128)S(1)} %bitcast.50, s32[8,18432]{1,0:T(8,128)S(1)} %bitcast.49, bf16[8,18432]{1,0:T(8,128)(2,1)S(1)} %bitcast.51), kind=kOutput, calls=%fused_computation.10.clone.1 | convolution fusion | flops 266600448 | bytes 1507332 | tf_op jit(solution)/shard_map/while/body/eval_jaxpr/rcn,rbn->rbc/dot_general | solution.py:33
  248.2 1.2 fusion.29
  249.4 1.4 constant_dynamic-slice_fusion.5
  250.8 17.7 %fusion.30 = f32[16,8,4,200]{3,2,1,0:T(4,128)S(1)} fusion(f32[16,8,4,200]{3,2,1,0:T(4,128)S(1)} %get-tuple-element.150, s32[]{:T(128)} %get-tuple-element.149, s32[8,18432]{1,0:T(8,128)S(1)} %bitcast.50, s32[8,18432]{1,0:T(8,128)S(1)} %bitcast.49, bf16[8,18432]{1,0:T(8,128)(2,1)S(1)} %bitcast.51), kind=kOutput, calls=%fused_computation.10.clone.1 | convolution fusion | flops 266600448 | bytes 1507332 | tf_op jit(solution)/shard_map/while/body/eval_jaxpr/rcn,rbn->rbc/dot_general | solution.py:33
  272.0 1.2 fusion.29
  273.3 1.4 constant_dynamic-slice_fusion.5
  274.6 17.7 %fusion.30 = f32[16,8,4,200]{3,2,1,0:T(4,128)S(1)} fusion(f32[16,8,4,200]{3,2,1,0:T(4,128)S(1)} %get-tuple-element.150, s32[]{:T(128)} %get-tuple-element.149, s32[8,18432]{1,0:T(8,128)S(1)} %bitcast.50, s32[8,18432]{1,0:T(8,128)S(1)} %bitcast.49, bf16[8,18432]{1,0:T(8,128)(2,1)S(1)} %bitcast.51), kind=kOutput, calls=%fused_computation.10.clone.1 | convolution fusion | flops 266600448 | bytes 1507332 | tf_op jit(solution)/shard_map/while/body/eval_jaxpr/rcn,rbn->rbc/dot_general | solution.py:33
  295.8 1.2 fusion.29
  297.1 1.4 constant_dynamic-slice_fusion.5
  298.4 17.7 %fusion.30 = f32[16,8,4,200]{3,2,1,0:T(4,128)S(1)} fusion(f32[16,8,4,200]{3,2,1,0:T(4,128)S(1)} %get-tuple-element.150, s32[]{:T(128)} %get-tuple-element.149, s32[8,18432]{1,0:T(8,128)S(1)} %bitcast.50, s32[8,18432]{1,0:T(8,128)S(1)} %bitcast.49, bf16[8,18432]{1,0:T(8,128)(2,1)S(1)} %bitcast.51), kind=kOutput, calls=%fused_computation.10.clone.1 | convolution fusion | flops 266600448 | bytes 1507332 | tf_op jit(solution)/shard_map/while/body/eval_jaxpr/rcn,rbn->rbc/dot_general | solution.py:33
  319.6 1.2 fusion.29
  320.9 1.4 constant_dynamic-slice_fusion.5
  322.2 17.7 %fusion.30 = f32[16,8,4,200]{3,2,1,0:T(4,128)S(1)} fusion(f32[16,8,4,200]{3,2,1,0:T(4,128)S(1)} %get-tuple-element.150, s32[]{:T(128)} %get-tuple-element.149, s32[8,18432]{1,0:T(8,128)S(1)} %bitcast.50, s32[8,18432]{1,0:T(8,128)S(1)} %bitcast.49, bf16[8,18432]{1,0:T(8,128)(2,1)S(1)} %bitcast.51), kind=kOutput, calls=%fused_computation.10.clone.1 | convolution fusion | flops 266600448 | bytes 1507332 | tf_op jit(solution)/shard_map/while/body/eval_jaxpr/rcn,rbn->rbc/dot_general | solution.py:33
  343.5 1.2 fusion.29
  344.7 1.4 constant_dynamic-slice_fusion.5
  346.1 17.7 %fusion.30 = f32[16,8,4,200]{3,2,1,0:T(4,128)S(1)} fusion(f32[16,8,4,200]{3,2,1,0:T(4,128)S(1)} %get-tuple-element.150, s32[]{:T(128)} %get-tuple-element.149, s32[8,18432]{1,0:T(8,128)S(1)} %bitcast.50, s32[8,18432]{1,0:T(8,128)S(1)} %bitcast.49, bf16[8,18432]{1,0:T(8,128)(2,1)S(1)} %bitcast.51), kind=kOutput, calls=%fused_computation.10.clone.1 | convolution fusion | flops 266600448 | bytes 1507332 | tf_op jit(solution)/shard_map/while/body/eval_jaxpr/rcn,rbn->rbc/dot_general | solution.py:33
  367.2 1.1 fusion.29
  368.4 1.1 constant_dynamic-slice_fusion.5
  369.5 17.7 %fusion.30 = f32[16,8,4,200]{3,2,1,0:T(4,128)S(1)} fusion(f32[16,8,4,200]{3,2,1,0:T(4,128)S(1)} %get-tuple-element.150, s32[]{:T(128)} %get-tuple-element.149, s32[8,18432]{1,0:T(8,128)S(1)} %bitcast.50, s32[8,18432]{1,0:T(8,128)S(1)} %bitcast.49, bf16[8,18432]{1,0:T(8,128)(2,1)S(1)} %bitcast.51), kind=kOutput, calls=%fused_computation.10.clone.1 | convolution fusion | flops 266600448 | bytes 1507332 | tf_op jit(solution)/shard_map/while/body/eval_jaxpr/rcn,rbn->rbc/dot_general | solution.py:33
  387.2 0.9 copy.26
  388.1 34.0 %reduce-scatter.2.cloned.1.call-done = f32[4,200,16]{1,2,0:T(8,128)} async-done(((f32[4,200,128]{1,2,0:T(8,128)}), f32[4,200,16]{1,2,0:T(8,128)}) %reduce-scatter.2.cloned.1.call-update) | async-done | bytes 51216 | tf_op jit(solution)/shard_map/reduce_scatter | solution.py:42
  422.2 0.8 copy_bitcast_fusion.1
  423.0 2.3 reduce-window.6
  425.6 43.3 %all-gather = bf16[128,200,16]{1,2,0:T(8,128)(2,1)S(1)} all-gather(bf16[4,200,16]{1,2,0:T(8,128)(2,1)S(1)} %bitcast.56), channel_id=2, replica_groups=mesh['lat'=4,'lon'=8] {'lat','lon'}, dimensions={0}, use_global_device_ids=true | all-gather | bytes 844800 | tf_op jit(solution)/shard_map/all_gather | solution.py:44
  469.0 1.3 copy.20
  (50 shorter events, 17.1 us)
Async XLA Ops:
  6.5 415.6 %reduce-scatter.2.cloned.1.call-start = ((), (), s32[]{:S(2)}) async-start(), calls=%async_computation.1 | async-start | bytes 589824 | tf_op jit(solution)/shard_map/reduce_scatter | solution.py:42
Sparse Core Ops, SparseCore 0:
  388.3 33.8 reduce-scatter.1
